TPU v7x, 256 devices: a whole 4x4x8 slice. The times are simulated.
256 devices in a mesh: dp: 32 (over z, y), mp: 8 (over x, core).
Axes of the slice: x: 4, y: 4, z: 8, core: 2. Of those that a mesh axis runs over, the one named last changes fastest.
Arguments:
- queries: bfloat16 [4096, 8192], P('dp', 'mp'), may hold values from -8 to 8
- tree_keys: bfloat16 [4096, 1024], P('dp', 'mp'), may hold values from -18 to 18
- tree_values: bfloat16 [4096, 1024], P('dp', 'mp'), may hold values from -6 to 6
- cache_keys: bfloat16 [64, 4096, 1024], P('dp', None, 'mp'), may hold values from -8 to 8
- cache_values: bfloat16 [64, 4096, 1024], P('dp', None, 'mp'), may hold values from -6 to 6
- cache_lens: int32 [64], P('dp'), may hold values from 1024 to 4096, as said below
- parents: int32 [64, 64], P('dp'), may hold values from -1 to 62, as said below
- accepted_nodes: int32 [64, 8], P('dp'), may hold values from 0 to 63, as said below
- residual: bfloat16 [4096, 8192], P('dp', 'mp'), may hold values from -1.796875 to 1.796875
- out_weight: bfloat16 [8192, 8192], P('mp', 'dp'), may hold values from -0.0625 to 0.0625
Outputs:
- tree_hidden: bfloat16 [4096, 8192], P('dp', 'mp')
- accepted_hidden: bfloat16 [512, 8192], P(None, 'mp')
Inputs may be any that keep to these rules, and one draw needn't show every extreme that they name: parents[r, 0] = -1 and 0 <= parents[r, i] < i for i >= 1. accepted_nodes[r, 0] = 0, the nodes of a row increase, and parents[r, accepted_nodes[r, a + 1]] = accepted_nodes[r, a]. `cache_lens`: some request has exactly 4096 filled positions.
All inputs are finite; a program needn't handle non-finite values.
Results may differ from a plain program's by a relative error of at most 0.015.
Values may be sent and summed in bfloat16 or wider, within the bound.
A program may use at most 64 MiB of HBM per device.

v0:
```python
import math
import jax
import jax.numpy as jnp
from jax import lax
from jax.sharding import PartitionSpec as P

HEADS = 64
KV_HEADS = 8
HD = 128
neg_large = -1e30


def cut_along(value, dim, size):
    before, after = (value.shape[:dim], value.shape[dim + 1 :])
    return jnp.moveaxis(value.reshape(*before, size, -1, *after), dim, 0)


def summed_on_arrival(value, axis, dim):
    blocks = cut_along(value, dim, lax.axis_size(axis))
    arrived = lax.all_to_all(blocks, axis, split_axis=0, concat_axis=0, tiled=True)
    return arrived.astype(jnp.float32).sum(axis=0)


def sent_to_all(value, axis):
    size = lax.axis_size(axis)
    return lax.all_to_all(
        jnp.broadcast_to(value[None], (size, *value.shape)), axis, 0, 0, tiled=True
    )


def laid_out(blocks, dim):
    blocks = jnp.moveaxis(blocks, 0, dim)
    dims = blocks.shape
    return blocks.reshape(*dims[:dim], dims[dim] * dims[dim + 1], *dims[dim + 2 :])


def collect(value, axis, dim):
    blocks = sent_to_all(value, axis)
    return laid_out(blocks, dim)


def ancestry(parents, node_count):
    positions = jnp.arange(node_count, dtype=jnp.int32)
    parent_hot = (parents[:, :, None] == positions[None, None, :]).astype(jnp.float32)
    reached = parent_hot + jnp.eye(node_count, dtype=jnp.float32)[None]
    for squaring in range((node_count - 1).bit_length()):
        reached = jnp.minimum(
            jnp.einsum("rij,rjk->rik", reached, reached, precision=lax.Precision.HIGHEST), 1.0
        )
    return reached > 0.5


def per_device(
    queries,
    tree_keys,
    tree_values,
    cache_keys,
    cache_values,
    cache_lens,
    parents,
    accepted_nodes,
    residual,
    out_weight,
):
    request_count = parents.shape[0]
    node_count = parents.shape[1]
    cache_length = cache_keys.shape[1]
    kv_local = tree_keys.shape[1] // HD
    group_size = HEADS // KV_HEADS
    scale_factor = 1.0 / math.sqrt(HD)
    query_grid = queries.reshape(request_count, node_count, kv_local, group_size, HD)
    tree_key_grid = tree_keys.reshape(request_count, node_count, kv_local, HD)
    tree_value_grid = tree_values.reshape(request_count, node_count, kv_local, HD)
    cache_key_grid = cache_keys.reshape(request_count, cache_length, kv_local, HD)
    cache_value_grid = cache_values.reshape(request_count, cache_length, kv_local, HD)
    ancestor = ancestry(parents, node_count)
    tree_scores = (
        jnp.einsum(
            "rnkgd,rjkd->rnkgj", query_grid, tree_key_grid, preferred_element_type=jnp.float32
        )
        * scale_factor
    )
    tree_scores = jnp.where(ancestor[:, :, None, None, :], tree_scores, neg_large)
    run_max = jnp.max(tree_scores, axis=-1)
    tree_weights = jnp.exp(tree_scores - run_max[..., None])
    run_sum = jnp.sum(tree_weights, axis=-1)
    run_acc = jnp.einsum(
        "rnkgj,rjkd->rnkgd",
        tree_weights.astype(jnp.bfloat16),
        tree_value_grid,
        preferred_element_type=jnp.float32,
    )
    block_len = min(512, cache_length)

    def absorb(block_number, state_now):
        old_max, old_sum, old_acc = state_now
        block_start = block_number * block_len
        key_block = lax.dynamic_slice_in_dim(cache_key_grid, block_start, block_len, 1)
        value_block = lax.dynamic_slice_in_dim(cache_value_grid, block_start, block_len, 1)
        block_scores = (
            jnp.einsum(
                "rnkgd,rpkd->rnkgp", query_grid, key_block, preferred_element_type=jnp.float32
            )
            * scale_factor
        )
        positions = block_start + jnp.arange(block_len, dtype=jnp.int32)
        live_keys = positions[None, :] < cache_lens[:, None]
        block_scores = jnp.where(live_keys[:, None, None, None, :], block_scores, neg_large)
        new_max = jnp.maximum(old_max, jnp.max(block_scores, axis=-1))
        block_weights = jnp.exp(block_scores - new_max[..., None])
        rescale = jnp.exp(old_max - new_max)
        new_sum = old_sum * rescale + jnp.sum(block_weights, axis=-1)
        new_acc = old_acc * rescale[..., None] + jnp.einsum(
            "rnkgp,rpkd->rnkgd",
            block_weights.astype(jnp.bfloat16),
            value_block,
            preferred_element_type=jnp.float32,
        )
        return (new_max, new_sum, new_acc)

    trip_count = cache_length // block_len
    run_max, run_sum, run_acc = lax.fori_loop(0, trip_count, absorb, (run_max, run_sum, run_acc))
    attended = (run_acc / run_sum[..., None]).astype(jnp.bfloat16)
    attended = attended.reshape(request_count * node_count, kv_local * group_size * HD)
    partial_sum = jnp.dot(
        attended,
        lax.all_gather(out_weight, "dp", axis=1, tiled=True),
        preferred_element_type=jnp.float32,
    )
    own_share = summed_on_arrival(partial_sum.astype(jnp.bfloat16), "mp", 1)
    tree_hidden = (residual.astype(jnp.float32) + own_share).astype(jnp.bfloat16)
    row_base = jnp.arange(request_count, dtype=jnp.int32)[:, None] * node_count
    picked_rows = (row_base + accepted_nodes).reshape(-1)
    picked_hidden = jnp.take(tree_hidden, picked_rows, axis=0)
    accepted_hidden = collect(picked_hidden, "dp", 0)
    return (tree_hidden, accepted_hidden)


def solution(mesh):
    placed = (
        P("dp", "mp"),
        P("dp", "mp"),
        P("dp", "mp"),
        P("dp", None, "mp"),
        P("dp", None, "mp"),
        P("dp"),
        P("dp", None),
        P("dp", None),
        P("dp", "mp"),
        P("mp", "dp"),
    )
    return jax.shard_map(
        per_device,
        mesh=mesh,
        in_specs=placed,
        out_specs=(P("dp", "mp"), P(None, "mp")),
        check_vma=False,
    )
```

profile of v0, /device:TPU:8, one launch (start us, length us, event | category | flops | bytes accessed | tf_op | source)
XLA Modules:
  0.0 246.2 jit_solution(12301007341857706381)
XLA Ops:
  8.9 1.0 convolution_minimum_fusion.5
  12.2 31.6 %while.17 = (s32[]{:T(128)}, f32[2,64,1,8]{1,3,0,2:T(8,128)S(1)}, f32[2,64,1,8]{1,3,0,2:T(8,128)S(1)}, f32[2,64,1,8,128]{4,1,3,0,2:T(8,128)S(1)}, s32[2]{0:T(128...) while((s32[]{:T(128)}, f32[2,64,1,8]{1,3,0,2:T(8,128)S(1)}, ...), condition=%wide.region_5.6_spmd, body=%wide.region_2.5_spmd.sunk | while | flops 274469376 | bytes 8200375 | solution.py:122
  12.3 1.5 bitcast_reduce_fusion.2
  13.8 1.7 fusion.60
  16.3 1.5 bitcast_reduce_fusion.2
  17.8 1.7 fusion.60
  20.2 1.5 bitcast_reduce_fusion.2
  21.7 1.7 fusion.60
  24.2 1.5 bitcast_reduce_fusion.2
  25.7 1.7 fusion.60
  28.1 1.5 bitcast_reduce_fusion.2
  29.6 1.7 fusion.60
  32.1 1.5 bitcast_reduce_fusion.2
  33.6 1.7 fusion.60
  36.0 1.5 bitcast_reduce_fusion.2
  37.5 1.7 fusion.60
  40.0 1.5 bitcast_reduce_fusion.2
  41.5 1.7 fusion.60
  44.2 117.2 %all-gather.2.cloned.1.call-done = bf16[1024,8192]{1,0:T(8,128)(2,1)} async-done(((bf16[1024,256]{1,0:T(8,128)(2,1)}), bf16[1024,8192]{1,0:T(8,128)(2,1)}) %all-gather.2.cloned.1.call-update) | async-done | bytes 16777232 | tf_op jit(solution)/shard_map/all_gather | solution.py:127
  161.5 8.1 %convolution_convert_fusion = bf16[128,8192]{1,0:T(8,128)(2,1)S(1)} fusion(bf16[1024,8192]{1,0:T(8,128)(2,1)} %all-gather.2.cloned.1.call-done, bf16[16,8,8,128]{3,2,1,0:T(8,128)(2,1)S(1)} %bitcast.164), kind=kOutput, calls=%fused_computation.30 | convolution fusion | flops 2148532224 | bytes 19136512 | tf_op jit(solution)/shard_map/dot_general | solution.py:125
  169.6 1.5 copy.46
  171.1 4.4 %all-to-all-start = ((bf16[8,128,1024]{2,1,0:T(8,128)(2,1)}), bf16[8,128,1024]{2,1,0:T(8,128)(2,1)S(1)}, u32[]{:S(2)}, u32[]{:S(2)}) async-start(bf16[8,128,1024]{2,1,0:T(8,128)(2,1)} %bitcast.157), calls=%async_computation | async-start | bytes 4194304 | tf_op jit(solution)/shard_map/all_to_all | solution.py:20
  175.8 26.9 %all-to-all-done = bf16[8,128,1024]{2,1,0:T(8,128)(2,1)S(1)} async-done(((bf16[8,128,1024]{2,1,0:T(8,128)(2,1)}), bf16[8,128,1024]{2,1,0:T(8,128)(2,1)S(1)}, u32[]{:S(2)}, u32[]{:S(2)}) %all-to-all-start) | async-done | bytes 2097184 | tf_op jit(solution)/shard_map/all_to_all | solution.py:20
  203.9 34.5 %all_to_all.10 = bf16[32,16,1024]{2,1,0:T(8,128)(2,1)S(1)} all-to-all(bf16[32,16,1024]{2,1,0:T(8,128)(2,1)S(1)} %broadcast_in_dim.78), channel_id=1, replica_groups=mesh['dp'=32,'mp'=8] {'dp'}, dimensions={0} | all-to-all | bytes 2097152 | tf_op jit(solution)/shard_map/all_to_all | solution.py:26
  (91 shorter events, 12.6 us)
Async XLA Ops:
  7.2 4.7 %copy-start = (bf16[128,128]{1,0:T(8,128)(2,1)S(1)}, bf16[128,128]{1,0:T(8,128)(2,1)}, u32[]{:S(2)}) copy-start(bf16[128,128]{1,0:T(8,128)(2,1)} %param.14) | copy-start | bytes 98308
  7.2 3.9 %copy-start.3 = (bf16[128,128]{1,0:T(8,128)(2,1)S(1)}, bf16[128,128]{1,0:T(8,128)(2,1)}, u32[]{:S(2)}) copy-start(bf16[128,128]{1,0:T(8,128)(2,1)} %param.13) | copy-start | bytes 98308
  7.2 154.3 %all-gather.2.cloned.1.call-start = ((), (), s32[]{:S(2)}) async-start(), calls=%async_computation.2 | async-start | bytes 17301504 | tf_op jit(solution)/shard_map/all_gather | solution.py:127
  11.1 1.1 copy-start.4
  171.1 4.4 %copy-start.5 = (s32[2,8]{1,0:T(2,128)S(1)}, s32[2,8]{1,0:T(2,128)}, u32[]{:S(2)}) copy-start(s32[2,8]{1,0:T(2,128)} %param.19) | copy-start | bytes 196
  171.1 31.6 %all-to-all-start = ((bf16[8,128,1024]{2,1,0:T(8,128)(2,1)}), bf16[8,128,1024]{2,1,0:T(8,128)(2,1)S(1)}, u32[]{:S(2)}, u32[]{:S(2)}) async-start(bf16[8,128,1024]{2,1,0:T(8,128)(2,1)} %bitcast.157), calls=%async_computation | async-start | bytes 4194304 | tf_op jit(solution)/shard_map/all_to_all | solution.py:20
  175.5 27.5 %copy-start.2 = (bf16[128,1024]{1,0:T(8,128)(2,1)S(1)}, bf16[128,1024]{1,0:T(8,128)(2,1)}, u32[]{:S(2)}) copy-start(bf16[128,1024]{1,0:T(8,128)(2,1)} %param.20) | copy-start | bytes 786436
  203.1 36.3 %copy-start.1 = (bf16[128,1024]{1,0:T(8,128)(2,1)}, bf16[128,1024]{1,0:T(8,128)(2,1)S(1)}, u32[]{:S(2)}) copy-start(bf16[128,1024]{1,0:T(8,128)(2,1)S(1)} %add_convert_fusion) | copy-start | bytes 786436
Sparse Core Ops, SparseCore 0:
  10.5 150.9 all-gather.1
where the time goes:
time: 247 us; the launch traced here: 246 us
  waiting for transfers between devices  145 us (59%)
  matrix products  36 us (15%)
  blocking collectives  34.5 us (14%)
  between operations  14.3 us (6%)
  other arithmetic  6.76 us (3%)
  local copies, waits for them, and re-layouts  5.06 us (2%)
  starting transfers between devices  4.42 us (2%)
    all_gather x1, waiting for transfers between devices, per_device(): lax.all_gather(out_weight, 'dp', axis=1, tiled=True)  117 us
    all_to_all x1, blocking collectives, sent_to_all(): lax.all_to_all(jnp.broadcast_to(value[None], (size, *value.shape)), axis,...  34.5 us
    all_to_all x1, waiting for transfers between devices, summed_on_arrival(): lax.all_to_all(blocks, axis, split_axis=0, concat_axis=0, tiled=True)  26.9 us
    dot_general x8, matrix products, absorb(): jnp.einsum('rnkgp,rpkd->rnkgd', block_weights.astype(jnp.bfloat16), value...  13.5 us
    dot_general x8, matrix products, absorb(): jnp.einsum('rnkgd,rpkd->rnkgp', query_grid, key_block, preferred_element_...  11.7 us
    dot_general x1, matrix products, per_device(): jnp.dot(attended, lax.all_gather(out_weight, 'dp', axis=1, tiled=True), p...  8.12 us
    reduce_sum x8, other arithmetic, absorb(): new_sum = old_sum * rescale + jnp.sum(block_weights, axis=-1)  5.06 us
  transfers between devices with their start and end apart: 2, of which 2 were waited for; matrix products, arithmetic and copies ran while one was open for 15% of the time, Pallas kernels for 0%

commit v1 on v0

--- a/solution.py
+++ b/solution.py
@@ -8,6 +8,13 @@
 KV_HEADS = 8
 HD = 128
 neg_large = -1e30
+
+
+def all_by_exchange(x, axis, d):
+    count = lax.axis_size(axis)
+    blocks = jnp.stack([x for _ in range(count)])
+    blocks = lax.all_to_all(blocks, axis, split_axis=0, concat_axis=0)
+    return jnp.concatenate(blocks, axis=d)
 
 
 def cut_along(value, dim, size):
@@ -123,9 +130,7 @@
     attended = (run_acc / run_sum[..., None]).astype(jnp.bfloat16)
     attended = attended.reshape(request_count * node_count, kv_local * group_size * HD)
     partial_sum = jnp.dot(
-        attended,
-        lax.all_gather(out_weight, "dp", axis=1, tiled=True),
-        preferred_element_type=jnp.float32,
+        attended, all_by_exchange(out_weight, "dp", 1), preferred_element_type=jnp.float32
     )
     own_share = summed_on_arrival(partial_sum.astype(jnp.bfloat16), "mp", 1)
     tree_hidden = (residual.astype(jnp.float32) + own_share).astype(jnp.bfloat16)

time: 247 us -> 507 us (2.05)
  waiting for transfers between devices: 145 us -> 376 us
  blocking collectives: 34.5 us -> 55.8 us
  between operations: 14.3 us -> 0.9 us
  starting transfers between devices: 4.42 us -> 16.3 us
  local copies, waits for them, and re-layouts: 5.06 us -> 11.4 us
    all_to_all x0 -> x1, waiting for transfers between devices: none -> 349 us  [all_by_exchange(): blocks = lax.all_to_all(blocks, axis, split_axis=0, concat_axis=0)]
    all_gather x1 -> x0, waiting for transfers between devices: 117 us -> none  [per_device(): lax.all_gather(out_weight, 'dp', axis=1, tiled=True)]
    all_to_all x1, blocking collectives: 34.5 us -> 55.8 us  [sent_to_all(): lax.all_to_all(jnp.broadcast_to(value[None], (size, *value.shape)), axis,...]
    all_to_all x0 -> x1, starting transfers between devices: none -> 11.9 us  [all_by_exchange(): blocks = lax.all_to_all(blocks, axis, split_axis=0, concat_axis=0)]
    another operation x1 -> x2, local copies, waits for them, and re-layouts: 0.2 us -> 6.18 us  [the longest x1 5.99 us: all_by_exchange(): blocks = jnp.stack([x for _ in range(count)])]
  transfers between devices with their start and end apart: 2 -> 2, of which waited for: 2 -> 2; matrix products, arithmetic and copies ran while one was open for 15% -> 7% of each run, Pallas kernels for 0% -> 0%
where the time goes in v1:
time: 507 us; the launch traced here: 506 us
  waiting for transfers between devices  376 us (74%)
  blocking collectives  55.8 us (11%)
  matrix products  38.4 us (8%)
  starting transfers between devices  16.3 us (3%)
  local copies, waits for them, and re-layouts  11.4 us (2%)
  other arithmetic  6.76 us (1%)
    all_to_all x1, waiting for transfers between devices, all_by_exchange(): blocks = lax.all_to_all(blocks, axis, split_axis=0, concat_axis=0)  349 us
    all_to_all x1, blocking collectives, sent_to_all(): lax.all_to_all(jnp.broadcast_to(value[None], (size, *value.shape)), axis,...  55.8 us
    all_to_all x1, waiting for transfers between devices, summed_on_arrival(): lax.all_to_all(blocks, axis, split_axis=0, concat_axis=0, tiled=True)  26.9 us
    dot_general x8, matrix products, absorb(): jnp.einsum('rnkgp,rpkd->rnkgd', block_weights.astype(jnp.bfloat16), value...  13.5 us
    all_to_all x1, starting transfers between devices, all_by_exchange(): blocks = lax.all_to_all(blocks, axis, split_axis=0, concat_axis=0)  11.9 us
    dot_general x8, matrix products, absorb(): jnp.einsum('rnkgd,rpkd->rnkgp', query_grid, key_block, preferred_element_...  11.7 us
    dot_general x1, matrix products, per_device(): jnp.dot(attended, all_by_exchange(out_weight, 'dp', 1), preferred_element...  11.4 us
  transfers between devices with their start and end apart: 2, of which 2 were waited for; matrix products, arithmetic and copies ran while one was open for 7% of the time, Pallas kernels for 0%

profile of v1, /device:TPU:8, one launch (start us, length us, event | category | flops | bytes accessed | tf_op | source)
XLA Modules:
  0.0 505.9 jit_solution(15325253362405561197)
XLA Ops:
  1.9 6.0 %stack.2 = bf16[32,1024,256]{1,2,0:T(8,128)(2,1)} broadcast(bf16[1024,256]{0,1:T(8,128)(2,1)S(1)} %copy.29), dimensions={1,2} | broadcast | bytes 17301504 | tf_op jit(solution)/shard_map/stack | solution.py:15
  7.9 11.9 %all-to-all-start = ((bf16[32,1024,256]{1,2,0:T(8,128)(2,1)}), bf16[32,1024,256]{1,2,0:T(8,128)(2,1)}, u32[]{:S(2)}, u32[]{:S(2)}) async-start(bf16[32,1024,256]{1,2,0:T(8,128)(2,1)} %stack.2), calls=%async_computation | async-start | bytes 33554432 | tf_op jit(solution)/shard_map/all_to_all | solution.py:16
  22.4 31.5 %while.17 = (s32[]{:T(128)}, f32[2,64,1,8]{1,3,0,2:T(8,128)S(1)}, f32[2,64,1,8]{1,3,0,2:T(8,128)S(1)}, f32[2,64,1,8,128]{4,1,3,0,2:T(8,128)S(1)}, s32[2]{0:T(128...) while((s32[]{:T(128)}, f32[2,64,1,8]{1,3,0,2:T(8,128)S(1)}, ...), condition=%wide.region_5.6_spmd, body=%wide.region_2.5_spmd.sunk | while | flops 274469376 | bytes 8200383 | solution.py:129
  24.7 1.7 fusion.60
  26.5 1.5 bitcast_reduce_fusion.2
  28.6 1.7 fusion.60
  30.4 1.5 bitcast_reduce_fusion.2
  32.5 1.7 fusion.60
  34.3 1.5 bitcast_reduce_fusion.2
  36.5 1.7 fusion.60
  38.3 1.5 bitcast_reduce_fusion.2
  40.4 1.7 fusion.60
  42.2 1.5 bitcast_reduce_fusion.2
  44.4 1.7 fusion.60
  46.2 1.5 bitcast_reduce_fusion.2
  48.3 1.7 fusion.60
  50.1 1.5 bitcast_reduce_fusion.2
  52.2 1.7 fusion.60
  54.3 348.9 %all-to-all-done = bf16[32,1024,256]{1,2,0:T(8,128)(2,1)} async-done(((bf16[32,1024,256]{1,2,0:T(8,128)(2,1)}), bf16[32,1024,256]{1,2,0:T(8,128)(2,1)}, u32[]{:S(2)}, u32[]{:S(2)}) %all-to-all-start) | async-done | bytes 16777248 | tf_op jit(solution)/shard_map/all_to_all | solution.py:16
  403.3 11.4 %convolution_convert_fusion = bf16[128,8192]{1,0:T(8,128)(2,1)S(1)} fusion(bf16[1024,8192]{0,1:T(8,128)(2,1)} %bitcast.34, bf16[16,8,8,128]{3,2,1,0:T(8,128)(2,1)S(1)} %bitcast.166), kind=kOutput, calls=%fused_computation.30 | convolution fusion | flops 2148532224 | bytes 19136512 | tf_op jit(solution)/shard_map/dot_general | solution.py:132
  414.7 1.6 copy.48
  416.3 4.4 all-to-all-start.1
  421.0 26.9 %all-to-all-done.1 = bf16[8,128,1024]{2,1,0:T(8,128)(2,1)S(1)} async-done(((bf16[8,128,1024]{2,1,0:T(8,128)(2,1)}), bf16[8,128,1024]{2,1,0:T(8,128)(2,1)S(1)}, u32[]{:S(2)}, u32[]{:S(2)}) %all-to-all-start.1) | async-done | bytes 2097184 | tf_op jit(solution)/shard_map/all_to_all | solution.py:27
  449.1 55.8 %all_to_all.15 = bf16[32,16,1024]{2,1,0:T(8,128)(2,1)S(1)} all-to-all(bf16[32,16,1024]{2,1,0:T(8,128)(2,1)S(1)} %broadcast_in_dim.78), channel_id=1, replica_groups=mesh['dp'=32,'mp'=8] {'dp'}, dimensions={0} | all-to-all | bytes 2097152 | tf_op jit(solution)/shard_map/all_to_all | solution.py:33
  (96 shorter events, 13.9 us)
Async XLA Ops:
  0.6 21.4 %copy-start = (bf16[128,128]{1,0:T(8,128)(2,1)S(1)}, bf16[128,128]{1,0:T(8,128)(2,1)}, u32[]{:S(2)}) copy-start(bf16[128,128]{1,0:T(8,128)(2,1)} %param.14) | copy-start | bytes 98308
  7.9 11.9 %copy-start.2 = (bf16[128,1024]{1,0:T(8,128)(2,1)S(1)}, bf16[128,1024]{1,0:T(8,128)(2,1)}, u32[]{:S(2)}) copy-start(bf16[128,1024]{1,0:T(8,128)(2,1)} %param.12) | copy-start | bytes 786436
  7.9 12.0 %copy-start.6 = (s32[2,64]{1,0:T(2,128)S(1)}, s32[2,64]{1,0:T(2,128)}, u32[]{:S(2)}) copy-start(s32[2,64]{1,0:T(2,128)} %param.18) | copy-start | bytes 1540
  7.9 13.4 %copy-start.4 = (bf16[128,128]{1,0:T(8,128)(2,1)S(1)}, bf16[128,128]{1,0:T(8,128)(2,1)}, u32[]{:S(2)}) copy-start(bf16[128,128]{1,0:T(8,128)(2,1)} %param.13) | copy-start | bytes 98308
  7.9 395.4 %all-to-all-start = ((bf16[32,1024,256]{1,2,0:T(8,128)(2,1)}), bf16[32,1024,256]{1,2,0:T(8,128)(2,1)}, u32[]{:S(2)}, u32[]{:S(2)}) async-start(bf16[32,1024,256]{1,2,0:T(8,128)(2,1)} %stack.2), calls=%async_computation | async-start | bytes 33554432 | tf_op jit(solution)/shard_map/all_to_all | solution.py:16
  21.3 1.1 copy-start.5
  416.3 4.4 copy-start.7
  416.3 31.6 %all-to-all-start.1 = ((bf16[8,128,1024]{2,1,0:T(8,128)(2,1)}), bf16[8,128,1024]{2,1,0:T(8,128)(2,1)S(1)}, u32[]{:S(2)}, u32[]{:S(2)}) async-start(bf16[8,128,1024]{2,1,0:T(8,128)(2,1)} %bitcast.159), calls=%async_computation.1 | async-start | bytes 4194304 | tf_op jit(solution)/shard_map/all_to_all | solution.py:27
  420.7 27.5 %copy-start.3 = (bf16[128,1024]{1,0:T(8,128)(2,1)S(1)}, bf16[128,1024]{1,0:T(8,128)(2,1)}, u32[]{:S(2)}) copy-start(bf16[128,1024]{1,0:T(8,128)(2,1)} %param.20) | copy-start | bytes 786436
  448.3 57.6 %copy-start.1 = (bf16[128,1024]{1,0:T(8,128)(2,1)}, bf16[128,1024]{1,0:T(8,128)(2,1)S(1)}, u32[]{:S(2)}) copy-start(bf16[128,1024]{1,0:T(8,128)(2,1)S(1)} %add_convert_fusion) | copy-start | bytes 786436
